TPU v7x, 32 devices: a whole 2x2x4 slice. The times are simulated.
32 devices in a mesh: gx: 4 (over y, core), gy: 8 (over z, x).
Axes of the slice: x: 2, y: 2, z: 4, core: 2. Of those that a mesh axis runs over, the one named last changes fastest.
Arguments:
- offsets: float32 [2, 8, 64, 128], P(None, 'gx', 'gy'), may hold values from 0 to 1
- masses: float32 [8, 64, 128], P('gx', 'gy'), may hold values from 0.01 to 0.04
- counts: int32 [8, 64], P('gx', 'gy'), may hold values from 1 to 128, as said below
- source: float32 [8, 64, 128], P('gx', 'gy'), may hold values from -6 to 6
Outputs:
- density: float32 [8, 64, 128], P('gx', 'gy')
- pressure: float32 [8, 64, 128], P('gx', 'gy')
- residual: float32 [8, 64, 128], P('gx', 'gy')
- peaks: float32 [5], replicated
Inputs may be any that keep to these rules, and one draw needn't show every extreme that they name: `counts`: each cell's occupied slots come first; some cell holds 128 particles.
All inputs are finite; a program needn't handle non-finite values.
Results may differ from a plain program's by a relative error of at most 0.0003.
Values sent between devices are 32-bit elements; how exact they have to be, the bound alone decides.
A program may use at most 64 MiB of HBM per device.

v0:
```python
import functools

import jax
import jax.numpy as jnp
from jax import lax
from jax.experimental import pallas as pl
from jax.experimental.pallas import tpu as pltpu
from jax.sharding import PartitionSpec as P

ITERS = 5
BASE_STIFF = 0.5
PAIR_SCALE = 0.05
NEIGHBOUR_STEPS = [(step_x, step_y) for step_x in (-1, 0, 1) for step_y in (-1, 0, 1)]
SIDES = [step for step in NEIGHBOUR_STEPS if step != (0, 0)]
MESH = pl.DeviceIdType.MESH
SUMS = 8


def own_edge(step, count):
    return {1: pl.ds(count - 1, 1), -1: pl.ds(0, 1), 0: pl.ds(0, count)}[step]


def halo_edge(step, count):
    return {1: pl.ds(0, 1), -1: pl.ds(count + 1, 1), 0: pl.ds(1, count)}[step]


def inner_edge(step, count):
    return {1: pl.ds(count, 1), -1: pl.ds(1, 1), 0: pl.ds(1, count)}[step]


def kernel(
    size_x, size_y, row_count, col_count,
    fields_ref, rows_ref,
    density_ref, pressure_ref, residual_ref, peaks_ref,
    pad_fields, pad_density, pad_vector, weights, gather_x, gather_y, direction_ref, along_ref,
    field_send, field_recv, density_send, density_recv, vector_send, vector_recv,
    send_x, recv_x, send_y, recv_y,
):
    here_x, here_y = lax.axis_index("gx"), lax.axis_index("gy")
    cell_count = row_count * col_count
    slots = rows_ref.shape[-1]

    for pad in (pad_fields, pad_density):
        pad[...] = jnp.zeros_like(pad)
    for step in range(ITERS):
        pad_vector[step] = jnp.zeros(pad_vector.shape[1:], jnp.float32)

    low_x, high_x = (here_x > 0), (here_x < size_x - 1)
    low_y, high_y = (here_y > 0), (here_y < size_y - 1)

    def there(step, low, high):
        return {1: high, -1: low}[step]

    def on_side(step_x, step_y, action):
        conditions = []
        if step_x:
            conditions.append(there(step_x, low_x, high_x))
        if step_y:
            conditions.append(there(step_y, low_y, high_y))
        condition = conditions[0]
        for other in conditions[1:]:
            condition = jnp.logical_and(condition, other)
        pl.when(condition)(action)

    barrier = pltpu.get_barrier_semaphore()

    def greet(device):
        pl.semaphore_signal(barrier, inc=1, device_id=device, device_id_type=MESH)

    for ahead in range(1, size_x):
        greet((lax.rem(here_x + ahead, size_x), here_y))
    for ahead in range(1, size_y):
        greet((here_x, lax.rem(here_y + ahead, size_y)))
    for step_x, step_y in SIDES:
        if step_x and step_y:
            on_side(step_x, step_y, functools.partial(greet, (here_x + step_x, here_y + step_y)))
    as_int = lambda flag: flag.astype(jnp.int32)
    corners = (as_int(low_x) + as_int(high_x)) * (as_int(low_y) + as_int(high_y))
    pl.semaphore_wait(barrier, size_x - 1 + size_y - 1 + corners)

    def halo_copy(side, source_of, target, send_sem, recv_sem):
        step_x, step_y = SIDES[side]
        return pltpu.make_async_remote_copy(
            src_ref=source_of(step_x, step_y),
            dst_ref=target.at[halo_edge(step_x, row_count), halo_edge(step_y, col_count)],
            send_sem=send_sem.at[side],
            recv_sem=recv_sem.at[side],
            device_id=(here_x + step_x, here_y + step_y),
            device_id_type=MESH,
        )

    def inner_of(pad):
        return lambda step_x, step_y: pad.at[
            inner_edge(step_x, row_count), inner_edge(step_y, col_count)
        ]

    def start_exchange(*args):
        for side, (step_x, step_y) in enumerate(SIDES):
            on_side(step_x, step_y, lambda side=side: halo_copy(side, *args).start())

    def end_exchange(*args):
        for side, (step_x, step_y) in enumerate(SIDES):
            on_side(-step_x, -step_y, lambda side=side: halo_copy(side, *args).wait_recv())
        for side, (step_x, step_y) in enumerate(SIDES):
            on_side(step_x, step_y, lambda side=side: halo_copy(side, *args).wait_send())

    lanes = lax.broadcasted_iota(jnp.int32, (slots, slots), 1)

    def as_columns(rows):
        filler = jnp.zeros((slots - cell_count, slots), jnp.float32)
        return jnp.concatenate([rows, filler], axis=0).T

    def as_rows(columns):
        return columns.T[:cell_count]

    def column(columns, cell):
        return jnp.sum(jnp.where(lanes == cell, columns, 0.0), axis=1, keepdims=True)

    def over_cells(terms):
        def one(cell, columns):
            total = terms(cell, lax.div(cell, col_count) + 1, lax.rem(cell, col_count) + 1)
            return jnp.where(lanes == cell, jnp.sum(total, axis=1, keepdims=True), columns)

        return lax.fori_loop(0, cell_count, one, jnp.zeros((slots, slots), jnp.float32))

    def put_rows(rows, pad):
        for cell in range(cell_count):
            pad[cell // col_count + 1, cell % col_count + 1] = rows[cell : cell + 1]

    field_args = (
        lambda step_x, step_y: fields_ref.at[
            own_edge(step_x, row_count), own_edge(step_y, col_count)
        ],
        pad_fields, field_send, field_recv,
    )
    start_exchange(*field_args)
    pad_fields[pl.ds(1, row_count), pl.ds(1, col_count)] = fields_ref[...]
    columns_x, columns_y = as_columns(rows_ref[0]), as_columns(rows_ref[1])
    occupied = rows_ref[2]
    end_exchange(*field_args)

    def density_terms(cell, at_x, at_y):
        own_x, own_y = column(columns_x, cell), column(columns_y, cell)
        total = jnp.zeros((slots, slots), jnp.float32)
        for index, (step_x, step_y) in enumerate(NEIGHBOUR_STEPS):
            near = pad_fields[at_x + step_x, at_y + step_y]
            offset_x = (step_x + near[0:1]) - own_x
            offset_y = (step_y + near[1:2]) - own_y
            falloff = jnp.maximum(1.0 - (offset_x * offset_x + offset_y * offset_y), 0.0)
            square = falloff * falloff
            weights[cell, index] = square
            total = total + square * falloff * near[2:3]
        return total

    density = 1.0 + as_rows(over_cells(density_terms))
    density_ref[...] = density
    put_rows(density, pad_density)

    density_args = (inner_of(pad_density), pad_density, density_send, density_recv)
    start_exchange(*density_args)
    columns_density = as_columns(density)
    end_exchange(*density_args)

    def weight_terms(cell, at_x, at_y):
        own_density = column(columns_density, cell)
        total = jnp.zeros((slots, slots), jnp.float32)
        for index, (step_x, step_y) in enumerate(NEIGHBOUR_STEPS):
            near = pad_fields[at_x + step_x, at_y + step_y]
            near_density = pad_density[at_x + step_x, at_y + step_y]
            weight = weights[cell, index] * ((2.0 * PAIR_SCALE) / (own_density + near_density))
            weights[cell, index] = weight
            total = total + weight * near[3:4]
        return total

    diagonal = BASE_STIFF + occupied * as_rows(over_cells(weight_terms))

    message_row = lax.broadcasted_iota(jnp.int32, (SUMS, slots), 0)

    def spread(parts, index, size, here, gather, send_sem, recv_sem, axis):
        slot = gather.at[index]
        slot[here] = parts

        def copy(ahead, owner):
            peer = lax.rem(here + ahead, size)
            return pltpu.make_async_remote_copy(
                src_ref=slot.at[here],
                dst_ref=slot.at[owner(peer)],
                send_sem=send_sem.at[ahead],
                recv_sem=recv_sem.at[index, owner(peer)],
                device_id=(peer, here_y) if axis == 0 else (here_x, peer),
                device_id_type=MESH,
            )

        for ahead in range(1, size):
            copy(ahead, lambda peer: here).start()
        for ahead in range(1, size):
            copy(ahead, lambda peer: peer).wait_recv()
        for ahead in range(1, size):
            copy(ahead, lambda peer: here).wait_send()
        summed = largest = slot[0]
        for other in range(1, size):
            summed = summed + slot[other]
            largest = jnp.maximum(largest, slot[other])
        return jnp.where(message_row == 2, largest, summed)

    def reduced(index, first, second, magnitude):
        total = lambda rows: jnp.sum(rows, axis=0, keepdims=True)
        peak = jnp.max(magnitude, axis=0, keepdims=True)
        parts = jnp.where(
            message_row == 0,
            total(first),
            jnp.where(message_row == 1, total(second), jnp.where(message_row == 2, peak, 0.0)),
        )
        parts = spread(parts, index, size_x, here_x, gather_x, send_x, recv_x, 0)
        parts = spread(parts, index, size_y, here_y, gather_y, send_y, recv_y, 1)
        sums = jnp.sum(parts, axis=1, keepdims=True)
        peaks = jnp.max(parts, axis=1, keepdims=True)
        wide = lambda one: jnp.broadcast_to(one, (1, slots))
        return wide(sums[0:1]), wide(sums[1:2]), wide(peaks[2:3])

    pressure_ref[...] = jnp.zeros_like(pressure_ref)
    residual_ref[...] = rows_ref[3] * occupied
    direction_ref[...] = jnp.zeros_like(direction_ref)
    along_ref[...] = jnp.zeros_like(along_ref)
    peaks_ref[...] = jnp.zeros_like(peaks_ref)

    def iteration(step, carry):
        precond_now, step_size = carry
        residual = residual_ref[...]
        scaled = residual / diagonal
        pad = pad_vector.at[step]
        put_rows(scaled, pad)
        args = (inner_of(pad), pad, vector_send, vector_recv.at[step])
        start_exchange(*args)
        end_exchange(*args)

        def vector_terms(cell, at_x, at_y):
            total = jnp.zeros((slots, slots), jnp.float32)
            for index, (step_x, step_y) in enumerate(NEIGHBOUR_STEPS):
                total = total + weights[cell, index] * pad[at_x + step_x, at_y + step_y]
            return total

        image = diagonal * scaled - occupied * as_rows(over_cells(vector_terms))
        precond_next, curvature, peak = reduced(
            step, residual * scaled, scaled * image, jnp.abs(residual)
        )
        peaks_ref[pl.ds(step, 1)] = peak
        ratio = jnp.where(step == 0, 0.0, precond_next / precond_now)
        step_size = precond_next / (curvature - ratio * precond_next / step_size)
        direction = scaled + ratio * direction_ref[...]
        along = image + ratio * along_ref[...]
        direction_ref[...] = direction
        along_ref[...] = along
        pressure_ref[...] = pressure_ref[...] + step_size * direction
        residual_ref[...] = residual - step_size * along
        return precond_next, step_size

    ones = jnp.ones((1, slots), jnp.float32)
    lax.fori_loop(0, ITERS, iteration, (ones, ones))
    magnitude = jnp.abs(residual_ref[...])
    peaks_ref[pl.ds(ITERS, 1)] = reduced(ITERS, magnitude, magnitude, magnitude)[2]


def body(size_x, size_y, offsets, masses, counts, source):
    row_count, col_count, slots = masses.shape
    cell_count = row_count * col_count
    occupied = (jnp.arange(slots, dtype=jnp.int32)[None, None, :] < counts[:, :, None]).astype(
        jnp.float32
    )
    fields = jnp.stack([offsets[0], offsets[1], masses * occupied, occupied], axis=2)
    rows = jnp.stack([offsets[0], offsets[1], occupied, source]).reshape(4, cell_count, slots)
    padded = (row_count + 2, col_count + 2)
    dma, f32, sides = pltpu.SemaphoreType.DMA, jnp.float32, len(SIDES)
    vmem = pl.BlockSpec(memory_space=pltpu.VMEM)
    block = jax.ShapeDtypeStruct((cell_count, slots), f32)
    density, pressure, residual, peaks = pl.pallas_call(
        functools.partial(kernel, size_x, size_y, row_count, col_count),
        out_shape=(block, block, block, jax.ShapeDtypeStruct((8, slots), f32)),
        in_specs=[vmem] * 2,
        out_specs=(vmem,) * 4,
        scratch_shapes=[
            pltpu.VMEM(padded + (4, slots), f32),
            pltpu.VMEM(padded + (1, slots), f32),
            pltpu.VMEM((ITERS,) + padded + (1, slots), f32),
            pltpu.VMEM((cell_count, len(NEIGHBOUR_STEPS), slots, slots), f32),
            pltpu.VMEM((ITERS + 1, size_x, SUMS, slots), f32),
            pltpu.VMEM((ITERS + 1, size_y, SUMS, slots), f32),
            pltpu.VMEM((cell_count, slots), f32),
            pltpu.VMEM((cell_count, slots), f32),
            dma((sides,)), dma((sides,)),
            dma((sides,)), dma((sides,)),
            dma((sides,)), dma((ITERS, sides)),
            dma((size_x,)), dma((ITERS + 1, size_x)),
            dma((size_y,)), dma((ITERS + 1, size_y)),
        ],
        compiler_params=pltpu.CompilerParams(collective_id=0, has_side_effects=True),
    )(fields, rows)
    shape = (row_count, col_count, slots)
    return (
        density.reshape(shape),
        pressure.reshape(shape),
        residual.reshape(shape),
        peaks[1 : ITERS + 1, 0],
    )


def solution(mesh):
    in_specs = (P(None, "gx", "gy", None), P("gx", "gy", None), P("gx", "gy"), P("gx", "gy", None))
    out_specs = (P("gx", "gy", None), P("gx", "gy", None), P("gx", "gy", None), P())
    return jax.shard_map(
        functools.partial(body, mesh.shape["gx"], mesh.shape["gy"]),
        mesh=mesh, in_specs=in_specs, out_specs=out_specs, check_vma=False,
    )
```

profile of v0, /device:TPU:0, one launch (start us, length us, event | category | flops | bytes accessed | tf_op | source)
XLA Modules:
  0.0 96.7 jit_solution(258709774532795262)
XLA Ops:
  0.6 0.0 copy-start.1
  0.6 0.8 lt.49
  1.4 0.0 copy-start.6
  1.4 0.1 fusion.1
  1.5 0.0 copy-done.1
  1.5 0.6 copy-done.6
  2.1 0.0 copy-start
  2.1 0.1 fusion
  2.2 0.1 compare_convert_fusion
  2.2 0.6 copy-done
  2.8 0.0 copy-start.5
  2.8 0.6 pad_maximum_fusion.fields_ref
  3.4 0.1 copy-done.5
  3.5 0.6 pad_maximum_fusion.1.rows_ref
  4.1 89.3 %shard_map.75 = (f32[16,128]{1,0:T(8,128)}, f32[16,128]{1,0:T(8,128)}, f32[16,128]{1,0:T(8,128)}, f32[8,128]{1,0:T(8,128)}) custom-call(f32[2,8,4,128]{3,2,1,0:T(4,128)} %pad_maximum_fusion.fields_ref, f32[4,16,128]{2,1,0:T(8,128)} %pad_maximum_fusion.1.rows_ref), custom_call_target="tpu_custom_call" | custom-call | tf_op jit(solution)/shard_map/pallas_call | solution.py:276
  93.4 0.0 copy-start.7
  93.4 0.0 copy-start.4
  93.4 0.7 copy-done.7
  94.1 0.6 slice_reduce_fusion
  94.7 0.0 copy-done.4
  94.7 0.0 copy-start.3
  94.7 0.6 copy.11
  95.3 0.1 copy-done.3
  95.4 0.0 copy-start.2
  95.4 0.6 copy.12
  96.0 0.1 copy-done.2
  96.1 0.6 copy.13
  (1 shorter events, 0.0 us)
Async XLA Ops:
  0.6 0.9 copy-start.1
  1.4 0.7 copy-start.6
  2.1 0.7 copy-start
  2.8 0.7 copy-start.5
  93.4 0.7 copy-start.7
  93.4 1.3 %copy-start.4 = (f32[16,128]{1,0:T(8,128)S(1)}, f32[16,128]{1,0:T(8,128)}, u32[]{:S(2)}) copy-start(f32[16,128]{1,0:T(8,128)} %get-tuple-element.8) | copy-start | bytes 24580
  94.7 0.7 copy-start.3
  95.4 0.7 copy-start.2
where the time goes:
time: 97.2 us; the launch traced here: 96.7 us
  Pallas kernels  89.3 us (92%)
  local copies, waits for them, and re-layouts  5.29 us (5%)
  other arithmetic  1.47 us (2%)
    pallas_call x1, Pallas kernels, body(): pl.pallas_call(functools.partial(kernel, size_x, size_y, row_count, col_c...  89.3 us
    unnamed x19, local copies, waits for them, and re-layouts  3.89 us

commit v1 on v0

v1 whole, which is shorter than its diff:
```python
import functools

import jax
import jax.numpy as jnp
from jax import lax
from jax.experimental import pallas as pl
from jax.experimental.pallas import tpu as pltpu
from jax.sharding import PartitionSpec as P

ITERS = 5
BASE_STIFF = 0.5
PAIR_SCALE = 0.05
NEIGHBOUR_STEPS = [(step_x, step_y) for step_x in (-1, 0, 1) for step_y in (-1, 0, 1)]
SIDES = [step for step in NEIGHBOUR_STEPS if step != (0, 0)]
MESH = pl.DeviceIdType.MESH
FAR = 64.0
CENTRE, HALF = 0.4375, 0.5
CHUNK = 64


def two_sum(a, b):
    total = a + b
    part = total - a
    return total, (a - (total - part)) + (b - part)


def add(a, b):
    high, low = two_sum(a[0], b[0])
    return high, low + (a[1] + b[1])


def tidy(a):
    high = a[0] + a[1]
    return high, a[1] - (high - a[0])


def halves(a):
    wide = a * 4097.0
    high = wide - (wide - a)
    return high, a - high


def mul(a, b):
    a_high, a_low = halves(a[0])
    b_high, b_low = halves(b[0])
    product = a[0] * b[0]
    rest = ((a_high * b_high - product) + (a_high * b_low + a_low * b_high)) + a_low * b_low
    return tidy((product, rest + (a[0] * b[1] + a[1] * b[0])))


def neg(a):
    return -a[0], -a[1]


def sub(a, b):
    return tidy(add(a, neg(b)))


def inverse(a):
    first = 1.0 / a[0]
    start = (first, jnp.zeros_like(first))
    one = (jnp.ones_like(first), jnp.zeros_like(first))
    rest = sub(one, mul(start, a))
    return tidy((first, rest[0] * first))


def tree(items, combine):
    items = list(items)
    while len(items) > 1:
        paired = [combine(items[at], items[at + 1]) for at in range(0, len(items) - 1, 2)]
        items = paired + items[len(paired) * 2 :]
    return items[0]


def over_sublanes(pair, rows):
    shift = rows // 2
    while shift:
        pair = add(pair, tuple(pltpu.roll(part, shift, 0) for part in pair))
        shift //= 2
    return pair


def kernel(
    size_x, size_y, row_count, col_count,
    offsets_hbm, masses_hbm, counts_hbm, source_hbm,
    density_ref, pressure_ref, residual_ref, peaks_ref,
    offsets_ref, masses_ref, counts_ref, source_ref, load_sem,
    pad_fields, pad_density, pad_vector, weights, own_x, own_y, own_density,
    part, inverse_diag, diag_ref, vectors, products, images,
    gather_early, gather_late, gather_peak,
    field_send, field_recv, density_send, density_recv, vector_send, vector_recv,
    early_send, early_recv, late_send, late_recv, peak_send, peak_recv,
):
    here_x, here_y = lax.axis_index("gx"), lax.axis_index("gy")
    device_count = size_x * size_y
    slots = masses_ref.shape[-1]

    loads = [
        pltpu.make_async_copy(source, target, load_sem.at[index])
        for index, (source, target) in enumerate((
            (offsets_hbm, offsets_ref), (masses_hbm, masses_ref),
            (counts_hbm, counts_ref), (source_hbm, source_ref),
        ))
    ]
    for load in loads:
        load.start()

    low_x, high_x = (here_x > 0), (here_x < size_x - 1)
    low_y, high_y = (here_y > 0), (here_y < size_y - 1)

    def on_side(step_x, step_y, action):
        conditions = []
        if step_x:
            conditions.append({1: high_x, -1: low_x}[step_x])
        if step_y:
            conditions.append({1: high_y, -1: low_y}[step_y])
        condition = conditions[0]
        for other in conditions[1:]:
            condition = jnp.logical_and(condition, other)
        pl.when(condition)(action)

    def ahead(here, step, size):
        there = here + step
        return jnp.where(there >= size, there - size, there)

    def for_peers(action):
        if device_count <= 64:
            for index in range(1, device_count):
                action(index, index // size_y, index % size_y)
        else:
            def one(index, carry):
                action(index, lax.div(index, size_y), lax.rem(index, size_y))
                return carry

            lax.fori_loop(1, device_count, one, 0)

    barrier = pltpu.get_barrier_semaphore()

    def greet(device):
        pl.semaphore_signal(barrier, inc=1, device_id=device, device_id_type=MESH)

    near_only = max(size_x, size_y) <= ITERS + 3
    if near_only:
        for step_x, step_y in SIDES:
            on_side(step_x, step_y, functools.partial(greet, (here_x + step_x, here_y + step_y)))
    else:
        for_peers(lambda index, step_x, step_y: greet(
            (ahead(here_x, step_x, size_x), ahead(here_y, step_y, size_y))
        ))

    def fill(ref, value):
        ref[...] = jnp.full(ref.shape, value, jnp.float32)

    def fill_outside(at):
        fill(pad_fields.at[at], FAR)
        fill(pad_density.at[at], 0.0)
        for step in range(ITERS):
            fill(pad_vector.at[(step,) + at], 0.0)

    every = slice(None)
    pl.when(jnp.logical_not(low_x))(lambda: fill_outside((0, every)))
    pl.when(jnp.logical_not(high_x))(lambda: fill_outside((row_count + 1, every)))
    pl.when(jnp.logical_not(low_y))(lambda: fill_outside((every, 0)))
    pl.when(jnp.logical_not(high_y))(lambda: fill_outside((every, col_count + 1)))

    def halo_copy(side, pad, send_sem, recv_sem):
        step_x, step_y = SIDES[side]
        inner = lambda step, count: {1: pl.ds(count, 1), -1: pl.ds(1, 1), 0: pl.ds(1, count)}[step]
        outer = lambda step, count: {1: pl.ds(0, 1), -1: pl.ds(count + 1, 1), 0: pl.ds(1, count)}[step]
        return pltpu.make_async_remote_copy(
            src_ref=pad.at[inner(step_x, row_count), inner(step_y, col_count)],
            dst_ref=pad.at[outer(step_x, row_count), outer(step_y, col_count)],
            send_sem=send_sem.at[side],
            recv_sem=recv_sem.at[side],
            device_id=(here_x + step_x, here_y + step_y),
            device_id_type=MESH,
        )

    LONG = [side for side, step in enumerate(SIDES) if step[1]]
    SHORT = [side for side, step in enumerate(SIDES) if not step[1]]

    def start_halo(sides, *args):
        for side in sides:
            on_side(*SIDES[side], lambda side=side: halo_copy(side, *args).start())

    def end_halo(*args):
        for side, (step_x, step_y) in enumerate(SIDES):
            on_side(-step_x, -step_y, lambda side=side: halo_copy(side, *args).wait_recv())

    def end_sends(*args):
        for side, (step_x, step_y) in enumerate(SIDES):
            on_side(step_x, step_y, lambda side=side: halo_copy(side, *args).wait_send())

    def steps_of(row, place, inside):
        def is_inside(step_x, step_y):
            if not 0 <= row + step_x < row_count:
                return False
            return not (place == "first" and step_y < 0 or place == "last" and step_y > 0)

        return [
            (index, step_x, step_y)
            for index, (step_x, step_y) in enumerate(NEIGHBOUR_STEPS)
            if is_inside(step_x, step_y) == inside
        ]

    def edge_columns(action):
        for col, place in ((0, "first"), (col_count - 1, "last")):
            for row in range(row_count):
                action(row, col, place)

    def inner_columns(action):
        def one(col, carry):
            for row in range(row_count):
                action(row, col, "inner")
            return carry

        lax.fori_loop(1, col_count - 1, one, 0)

    def all_columns(action):
        edge_columns(action)
        inner_columns(action)

    def spread(row):
        return jnp.broadcast_to(row, (slots, slots)).T

    def gathered(total):
        return jnp.sum(total.T, axis=0, keepdims=True)

    def chunks(terms):
        return gathered(jnp.concatenate(
            [terms(pl.ds(start, CHUNK)) for start in range(0, slots, CHUNK)], axis=0
        ))

    for load in loads:
        load.wait()
    lane = lax.broadcasted_iota(jnp.int32, (col_count, slots), 1)
    square = (col_count, col_count)
    on_diagonal = lax.broadcasted_iota(jnp.int32, square, 0) == lax.broadcasted_iota(jnp.int32, square, 1)
    occupied = []
    for row in range(row_count):
        limits = jnp.where(
            on_diagonal, jnp.broadcast_to(counts_ref[row : row + 1].astype(jnp.float32), square), 0.0
        )
        limit = jnp.sum(limits, axis=1, keepdims=True)
        occupied.append((lane.astype(jnp.float32) < limit).astype(jnp.float32))
        live = occupied[row] > 0.0
        field_rows = (
            jnp.where(live, offsets_ref[0, row], FAR),
            jnp.where(live, offsets_ref[1, row], FAR),
            masses_ref[row],
            source_ref[row] * occupied[row],
        )
        source_ref[row] = field_rows[3]
        for col in range(col_count):
            for index in range(3):
                pad_fields[row + 1, col + 1, index : index + 1] = field_rows[index][col : col + 1]
        inverse_diag[row] = occupied[row].reshape(col_count, 1, slots)

    def spread_place(row, col, place):
        own_x[row, col] = spread(offsets_ref[0, row, pl.ds(col, 1)])
        own_y[row, col] = spread(offsets_ref[1, row, pl.ds(col, 1)])

    all_columns(spread_place)

    greeters = lambda low, high: low.astype(jnp.int32) + high.astype(jnp.int32)
    if near_only:
        count_x, count_y = greeters(low_x, high_x), greeters(low_y, high_y)
        pl.semaphore_wait(barrier, (count_x + 1) * (count_y + 1) - 1)
    else:
        pl.semaphore_wait(barrier, device_count - 1)

    field_args = (pad_fields, field_send, field_recv)
    start_halo(range(len(SIDES)), *field_args)

    def density_part(inside):
        def one(row, col, place):
            steps = steps_of(row, place, inside)

            def terms(rows):
                at_x, at_y = own_x[row, col, rows], own_y[row, col, rows]
                total = None
                for index, step_x, step_y in steps:
                    near = pad_fields[row + 1 + step_x, col + 1 + step_y]
                    offset_x = (step_x + near[0:1]) - at_x
                    offset_y = (step_y + near[1:2]) - at_y
                    falloff = jnp.maximum(1.0 - (offset_x * offset_x + offset_y * offset_y), 0.0)
                    squared = falloff * falloff
                    weights[row, col, index, rows] = squared
                    term = squared * falloff * near[2:3]
                    total = term if total is None else total + term
                return total

            return chunks(terms)

        return one

    def store_density_part(row, col, place):
        part[row, col] = density_part(True)(row, col, place)

    all_columns(store_density_part)
    end_halo(*field_args)

    def finish_density(row, col, place):
        density = 1.0 + (part[row, col] + density_part(False)(row, col, place))
        pad_density[row + 1, col + 1] = density
        density_ref[row, pl.ds(col, 1)] = density

    density_args = (pad_density, density_send, density_recv)
    edge_columns(finish_density)
    start_halo(LONG, *density_args)
    inner_columns(finish_density)
    start_halo(SHORT, *density_args)

    def weight_part(inside):
        def one(row, col, place):
            steps = steps_of(row, place, inside)

            def terms(rows):
                here = own_density[row, col, rows]
                total = None
                for index, step_x, step_y in steps:
                    there = pad_density[row + 1 + step_x, col + 1 + step_y]
                    weight = weights[row, col, index, rows] * ((2.0 * PAIR_SCALE) / (here + there))
                    weights[row, col, index, rows] = weight
                    total = weight if total is None else total + weight
                return total

            return chunks(terms)

        return one

    def store_weight_part(row, col, place):
        own_density[row, col] = spread(pad_density[row + 1, col + 1])
        part[row, col] = weight_part(True)(row, col, place)

    all_columns(store_weight_part)
    end_halo(*density_args)

    def finish_weights(row, col, place):
        occupied_row = inverse_diag[row, col]
        total = part[row, col] + weight_part(False)(row, col, place)
        diagonal = BASE_STIFF + occupied_row * total
        inverted = occupied_row / diagonal
        scaled = source_ref[row, pl.ds(col, 1)] * inverted
        diag_ref[row, pl.ds(col, 1)] = diagonal
        inverse_diag[row, col] = inverted
        vectors[0, row, pl.ds(col, 1)] = scaled
        pad_vector[0, row + 1, col + 1] = scaled

    def vector_args(step):
        return pad_vector.at[step], vector_send.at[step], vector_recv.at[step]

    edge_columns(finish_weights)
    start_halo(LONG, *vector_args(0))
    inner_columns(finish_weights)
    start_halo(SHORT, *vector_args(0))

    def product_part(step, inside):
        def one(row, col, place):
            total = None
            for index, step_x, step_y in steps_of(row, place, inside):
                term = weights[row, col, index] * pad_vector[step, row + 1 + step_x, col + 1 + step_y]
                total = term if total is None else total + term
            return gathered(total)

        return one

    def store_product_part(step):
        def one(row, col, place):
            part[row, col] = product_part(step, True)(row, col, place)

        return one

    def finish_product(step):
        def one(row, col, place):
            product = part[row, col] + product_part(step, False)(row, col, place)
            products[step, row, pl.ds(col, 1)] = product
            now = vectors[step, row, pl.ds(col, 1)]
            rest = inverse_diag[row, col] * product - CENTRE * now
            if step == 0:
                following = rest * (1.0 / HALF)
            else:
                following = rest * (2.0 / HALF) - vectors[step - 1, row, pl.ds(col, 1)]
            vectors[step + 1, row, pl.ds(col, 1)] = following
            if step + 1 < ITERS:
                pad_vector[step + 1, row + 1, col + 1] = following

        return one

    def set_image(step):
        for row in range(row_count):
            images[step, row] = diag_ref[row] * vectors[step, row] - products[step, row]

    def dot(left, right):
        zero = jnp.zeros((col_count, slots), jnp.float32)
        return tree([(left[row] * right[row], zero) for row in range(row_count)], add)

    def send_all(gather, send_sem, recv_sem):
        def one(index, step_x, step_y):
            return pltpu.make_async_remote_copy(
                src_ref=gather.at[0],
                dst_ref=gather.at[index],
                send_sem=send_sem.at[index],
                recv_sem=recv_sem.at[index],
                device_id=(ahead(here_x, step_x, size_x), ahead(here_y, step_y, size_y)),
                device_id_type=MESH,
            )

        return one

    def start_all(*args):
        for_peers(lambda *peer: send_all(*args)(*peer).start())

    def end_all(*args):
        for_peers(lambda *peer: send_all(*args)(*peer).wait_recv())

    def end_all_sends(*args):
        for_peers(lambda *peer: send_all(*args)(*peer).wait_send())

    early_args = (gather_early, early_send, early_recv)
    late_args = (gather_late, late_send, late_recv)
    peak_args = (gather_peak, peak_send, peak_recv)
    last = ITERS - 1
    group = slots // col_count
    entries = [("image", i, j) for j in range(ITERS) for i in range(j + 1) if i < last]
    entries += [("source", 0, j) for j in range(ITERS)]
    groups = -(-len(entries) // group)

    def early_sums():
        pairs = []
        for kind, i, j in entries:
            left = images.at[i] if kind == "image" else source_ref
            pairs.append(dot(left, vectors.at[j]))
        filler = jnp.zeros((col_count, slots), jnp.float32)
        for at in range(groups):
            rows = pairs[at * group : (at + 1) * group]
            rows = rows + [(filler, filler)] * (group - len(rows))
            flat = [jnp.concatenate([pair[which] for pair in rows], axis=0).T for which in (0, 1)]
            slabs = [
                (flat[0][start : start + 8], flat[1][start : start + 8]) for start in range(0, slots, 8)
            ]
            pair = over_sublanes(tree(slabs, add), 8)
            gather_early[0, at : at + 1] = pair[0][0:1]
            gather_early[0, groups + at : groups + at + 1] = pair[1][0:1]

    for step in range(ITERS):
        if step == last:
            early_sums()
            start_all(*early_args)
        all_columns(store_product_part(step))
        end_halo(*vector_args(step))
        edge_columns(finish_product(step))
        if step < last:
            start_halo(LONG, *vector_args(step + 1))
        inner_columns(finish_product(step))
        if step < last:
            start_halo(SHORT, *vector_args(step + 1))
        set_image(step)

    pair = over_sublanes(dot(images.at[last], vectors.at[last]), col_count)
    flat = [jnp.broadcast_to(part_of[0:1], (slots, slots)).T for part_of in pair]
    slabs = [(flat[0][start : start + 8], flat[1][start : start + 8]) for start in range(0, slots, 8)]
    pair = over_sublanes(tree(slabs, add), 8)
    gather_late[0, 0:1] = pair[0][0:1]
    gather_late[0, 1:2] = pair[1][0:1]
    start_all(*late_args)

    end_all(*early_args)
    sums = {}
    for at in range(groups):
        pair = tree(
            [
                (gather_early[device, at : at + 1], gather_early[device, groups + at : groups + at + 1])
                for device in range(device_count)
            ],
            add,
        )
        flat = [spread(part_of) for part_of in pair]
        for index, entry in enumerate(entries[at * group : (at + 1) * group]):
            rows = slice(index * col_count, (index + 1) * col_count)
            sums[entry] = tidy(over_sublanes((flat[0][rows], flat[1][rows]), col_count))
    matrix = lambda i, j: sums["image", min(i, j), max(i, j)]

    zero = jnp.zeros((col_count, slots), jnp.float32)
    nothing = (zero, zero)
    unit = (zero + 1.0, zero)
    number = lambda value: (zero + value, zero)
    inverses, factors, directions, shares = [], {}, [], []
    kept_last = None
    for k in range(ITERS):
        scaled = {}
        for j in range(k):
            value = matrix(k, j)
            for i in range(j):
                value = sub(value, mul(scaled[i], factors[j, i]))
            scaled[j] = value
            factors[k, j] = mul(value, inverses[j])
        target = sums["source", 0, k]
        for j in range(k):
            target = sub(target, mul(factors[k, j], shares[j][0]))
        removed = nothing
        for j in range(k):
            removed = tidy(add(removed, mul(scaled[j], factors[k, j])))
        direction = [nothing] * k + [unit]
        for j in range(k):
            for i in range(j + 1):
                direction[i] = sub(direction[i], mul(factors[k, j], directions[j][i]))
        directions.append(direction)
        if k < last:
            pivot = sub(matrix(k, k), removed)
            inverses.append(inverse(pivot))
            shares.append((target, mul(target, inverses[k])))
        else:
            kept_last = (target, removed)

    def applied(direction):
        count = len(direction)
        padded = direction + [nothing, nothing]
        out = []
        for i in range(count + 1):
            value = mul(padded[i], number(1.0 - CENTRE))
            if i:
                value = sub(value, mul(padded[i - 1], number(HALF if i == 1 else HALF / 2)))
            out.append(sub(value, mul(padded[i + 1], number(HALF / 2))))
        return out

    def combined(coefficients, row):
        return tree([value[0] * vectors[i, row] for i, value in enumerate(coefficients)], jnp.add)

    solution = [nothing] * ITERS
    remainder = [unit] + [nothing] * ITERS
    peak_rows = []

    def largest(rows):
        peak = tree([jnp.abs(one) for one in rows], jnp.maximum)
        return jnp.max(jnp.max(peak, axis=0, keepdims=True), axis=1, keepdims=True)

    for k in range(last):
        share = shares[k][1]
        image = applied(directions[k])
        for i, value in enumerate(directions[k]):
            solution[i] = tidy(add(solution[i], mul(share, value)))
        for i, value in enumerate(image):
            remainder[i] = sub(remainder[i], mul(share, value))
        rows = [diag_ref[row] * combined(remainder[: k + 2], row) for row in range(row_count)]
        peak_rows.append(largest(rows))
    residual_rows = rows
    image = applied(directions[last])
    solution_rows = [combined(solution[:last], row) for row in range(row_count)]
    direction_rows = [combined(directions[last], row) for row in range(row_count)]
    image_rows = [diag_ref[row] * combined(image, row) for row in range(row_count)]

    end_all(*late_args)
    pair = tree(
        [(gather_late[device, 0:1], gather_late[device, 1:2]) for device in range(device_count)], add
    )
    target, removed = kept_last
    pivot = sub(tidy(pair), (removed[0][0:1], removed[1][0:1]))
    share = target[0][0:1] / pivot[0]
    for row in range(row_count):
        residual_rows[row] = residual_rows[row] - share * image_rows[row]
        residual_ref[row] = residual_rows[row]
        pressure_ref[row] = solution_rows[row] + share * direction_rows[row]
    peak_rows.append(largest(residual_rows))
    lane = lax.broadcasted_iota(jnp.int32, (1, slots), 1)
    packed = jnp.zeros((1, slots), jnp.float32)
    for k in range(ITERS):
        packed = jnp.where(lane == k, peak_rows[k], packed)
    gather_peak[0] = packed
    start_all(*peak_args)

    end_sends(*field_args)
    end_sends(*density_args)
    for step in range(ITERS):
        end_sends(*vector_args(step))
    end_all_sends(*early_args)
    end_all_sends(*late_args)
    end_all(*peak_args)
    peaks_ref[...] = tree([gather_peak[device] for device in range(device_count)], jnp.maximum)
    end_all_sends(*peak_args)


def write_out(density_ref, pressure_ref, residual_ref, peaks_ref, *rest):
    outs, sems = rest[:3], rest[4]
    rest[3][...] = peaks_ref[0, : rest[3].shape[0]]
    copies = [
        pltpu.make_async_copy(source, target, sems.at[index])
        for index, (source, target) in enumerate(zip((density_ref, pressure_ref, residual_ref), outs))
    ]
    for copy in copies:
        copy.start()
    for copy in copies:
        copy.wait()


def body(size_x, size_y, offsets, masses, counts, source):
    row_count, col_count, slots = masses.shape
    devices = size_x * size_y
    padded = (row_count + 2, col_count + 2)
    block = (row_count, col_count, slots)
    dma, f32, sides = pltpu.SemaphoreType.DMA, jnp.float32, len(SIDES)
    scratch = lambda *shape: pltpu.VMEM(shape, f32)
    early_rows = 2 * (-(-(ITERS * (ITERS + 1) // 2 - 1 + ITERS) // (slots // col_count)))
    vmem = pl.BlockSpec(memory_space=pltpu.VMEM)
    hbm = pl.BlockSpec(memory_space=pl.ANY)
    shaped = jax.ShapeDtypeStruct(block, f32)
    results = pl.pallas_call(
        functools.partial(kernel, size_x, size_y, row_count, col_count),
        out_shape=(shaped, shaped, shaped, jax.ShapeDtypeStruct((1, slots), f32)),
        in_specs=[hbm] * 4,
        out_specs=(vmem,) * 4,
        scratch_shapes=[
            scratch(2, *block), scratch(*block), pltpu.VMEM((row_count, col_count), jnp.int32),
            scratch(*block), dma((4,)),
            scratch(*padded, 4, slots), scratch(*padded, 1, slots), scratch(ITERS, *padded, 1, slots),
            scratch(row_count, col_count, len(NEIGHBOUR_STEPS), slots, slots),
            scratch(row_count, col_count, slots, slots),
            scratch(row_count, col_count, slots, slots),
            scratch(row_count, col_count, slots, slots),
            scratch(row_count, col_count, 1, slots),
            scratch(row_count, col_count, 1, slots),
            scratch(*block),
            scratch(ITERS + 1, *block), scratch(ITERS, *block), scratch(ITERS, *block),
            scratch(devices, early_rows, slots), scratch(devices, 2, slots), scratch(devices, 1, slots),
            dma((sides,)), dma((sides,)), dma((sides,)), dma((sides,)),
            dma((ITERS, sides)), dma((ITERS, sides)),
            dma((devices,)), dma((devices,)), dma((devices,)), dma((devices,)),
            dma((devices,)), dma((devices,)),
        ],
        compiler_params=pltpu.CompilerParams(collective_id=0, has_side_effects=True),
    )(offsets, masses, counts, source)
    return pl.pallas_call(
        write_out,
        out_shape=(shaped, shaped, shaped, jax.ShapeDtypeStruct((ITERS,), f32)),
        in_specs=[vmem] * 4,
        out_specs=(hbm, hbm, hbm, vmem),
        scratch_shapes=[dma((3,))],
    )(*results)


def solution(mesh):
    in_specs = (P(None, "gx", "gy", None), P("gx", "gy", None), P("gx", "gy"), P("gx", "gy", None))
    out_specs = (P("gx", "gy", None), P("gx", "gy", None), P("gx", "gy", None), P())
    return jax.shard_map(
        functools.partial(body, mesh.shape["gx"], mesh.shape["gy"]),
        mesh=mesh, in_specs=in_specs, out_specs=out_specs, check_vma=False,
    )
```

time: 97.2 us -> 44.1 us (0.45)
  Pallas kernels: 89.3 us -> 43 us
  local copies, waits for them, and re-layouts: 5.29 us -> 0 us
  other arithmetic: 1.47 us -> 0 us
    pallas_call x1, Pallas kernels: 89.3 us -> 41.2 us  [body(): pl.pallas_call(functools.partial(kernel, size_x, size_y, row_count, col_c...]
    unnamed x19 -> x0, local copies, waits for them, and re-layouts: 3.89 us -> none
    pallas_call x0 -> x1, Pallas kernels: none -> 1.88 us  [body(): pl.pallas_call(write_out, out_shape=(shaped, shaped, shaped, jax.ShapeDty...]
    another operation x2 -> x0, other arithmetic: 1.24 us -> none  [the longest x1 0.63 us: body(): jnp.stack([offsets[0], offsets[1], masses * occupied, occupied], axis=2)]
where the time goes in v1:
time: 44.1 us; the launch traced here: 43.7 us
  Pallas kernels  43 us (98%)
  between operations  0.64 us (1%)
    pallas_call x1, Pallas kernels, body(): pl.pallas_call(functools.partial(kernel, size_x, size_y, row_count, col_c...  41.2 us
    pallas_call x1, Pallas kernels, body(): pl.pallas_call(write_out, out_shape=(shaped, shaped, shaped, jax.ShapeDty...  1.88 us

profile of v1, /device:TPU:0, one launch (start us, length us, event | category | flops | bytes accessed | tf_op | source)
XLA Modules:
  0.0 43.7 jit_solution(12976227153315753696)
XLA Ops:
  0.6 41.2 %shard_map.75 = (f32[2,8,128]{2,1,0:T(8,128)}, f32[2,8,128]{2,1,0:T(8,128)}, f32[2,8,128]{2,1,0:T(8,128)}, f32[1,128]{1,0:T(1,128)}) custom-call(f32[2,2,8,128]{3,2,1,0:T(8,128)} %offsets_hbm.1, f32[2,8,128]{2,1,0:T(8,128)} %masses_hbm.1, s32[2,8]{1,0:T(2,128)} %counts_hbm.1, f32[2,8,128]{2,1,0:T(8,128)} %source_hbm.1), custom_call_target="tpu_custom_call" | custom-call | tf_op jit(solution)/shard_map/pallas_call | solution.py:607
  41.8 1.9 %shard_map.76 = (f32[2,8,128]{2,1,0:T(8,128)}, f32[2,8,128]{2,1,0:T(8,128)}, f32[2,8,128]{2,1,0:T(8,128)}, f32[5]{0:T(128)}) custom-call(f32[2,8,128]{2,1,0:T(8,128)} %get-tuple-element.8.density_ref, f32[2,8,128]{2,1,0:T(8,128)} %get-tuple-element.9.pressure_ref, f32[2,8,128]{2,1,0:T(8,128)} %get-tuple-element.10.residual_ref, ...), custom_call_target="tpu_custom_call" | custom-call | tf_op jit(solution)/shard_map/pallas_call | solution.py:632

commit v2 on v1

--- a/solution.py
+++ b/solution.py
@@ -208,17 +208,21 @@
             for row in range(row_count):
                 action(row, col, place)
 
-    def inner_columns(action):
+    def inner_columns(action, unroll=True):
         def one(col, carry):
             for row in range(row_count):
                 action(row, col, "inner")
             return carry
 
-        lax.fori_loop(1, col_count - 1, one, 0)
-
-    def all_columns(action):
+        if unroll:
+            for col in range(1, col_count - 1):
+                one(col, 0)
+        else:
+            lax.fori_loop(1, col_count - 1, one, 0)
+
+    def all_columns(action, unroll=True):
         edge_columns(action)
-        inner_columns(action)
+        inner_columns(action, unroll)
 
     def spread(row):
         return jnp.broadcast_to(row, (slots, slots)).T
@@ -256,12 +260,6 @@
                 pad_fields[row + 1, col + 1, index : index + 1] = field_rows[index][col : col + 1]
         inverse_diag[row] = occupied[row].reshape(col_count, 1, slots)
 
-    def spread_place(row, col, place):
-        own_x[row, col] = spread(offsets_ref[0, row, pl.ds(col, 1)])
-        own_y[row, col] = spread(offsets_ref[1, row, pl.ds(col, 1)])
-
-    all_columns(spread_place)
-
     greeters = lambda low, high: low.astype(jnp.int32) + high.astype(jnp.int32)
     if near_only:
         count_x, count_y = greeters(low_x, high_x), greeters(low_y, high_y)
@@ -271,6 +269,12 @@
 
     field_args = (pad_fields, field_send, field_recv)
     start_halo(range(len(SIDES)), *field_args)
+
+    def spread_place(row, col, place):
+        own_x[row, col] = spread(offsets_ref[0, row, pl.ds(col, 1)])
+        own_y[row, col] = spread(offsets_ref[1, row, pl.ds(col, 1)])
+
+    all_columns(spread_place)
 
     def density_part(inside):
         def one(row, col, place):
@@ -443,28 +447,54 @@
             gather_early[0, at : at + 1] = pair[0][0:1]
             gather_early[0, groups + at : groups + at + 1] = pair[1][0:1]
 
-    for step in range(ITERS):
-        if step == last:
-            early_sums()
-            start_all(*early_args)
-        all_columns(store_product_part(step))
-        end_halo(*vector_args(step))
+    def sum_lanes(pair):
+        flat = [jnp.broadcast_to(part_of[0:1], (slots, slots)).T for part_of in pair]
+        slabs = [(flat[0][start : start + 8], flat[1][start : start + 8]) for start in range(0, slots, 8)]
+        return over_sublanes(tree(slabs, add), 8)
+
+    def end_product(step):
         edge_columns(finish_product(step))
         if step < last:
             start_halo(LONG, *vector_args(step + 1))
         inner_columns(finish_product(step))
         if step < last:
             start_halo(SHORT, *vector_args(step + 1))
-        set_image(step)
-
-    pair = over_sublanes(dot(images.at[last], vectors.at[last]), col_count)
-    flat = [jnp.broadcast_to(part_of[0:1], (slots, slots)).T for part_of in pair]
-    slabs = [(flat[0][start : start + 8], flat[1][start : start + 8]) for start in range(0, slots, 8)]
-    pair = over_sublanes(tree(slabs, add), 8)
+            set_image(step)
+
+    for step in range(last):
+        all_columns(store_product_part(step))
+        end_halo(*vector_args(step))
+        end_product(step)
+    early_sums()
+    start_all(*early_args)
+    all_columns(store_product_part(last))
+
+    for row in range(row_count):
+        for col in range(col_count):
+            own_x[row, col] = spread(vectors[last, row, pl.ds(col, 1)])
+            products[last, row, pl.ds(col, 1)] = part[row, col]
+    set_image(last)
+    inside_sum = dot(images.at[last], vectors.at[last])
+    end_halo(*vector_args(last))
+    crossing = []
+    for row in range(row_count):
+        for col in range(col_count):
+            place = "first" if col == 0 else "last" if col == col_count - 1 else "inner"
+            total = None
+            for index, step_x, step_y in steps_of(row, place, False):
+                term = weights[row, col, index] * pad_vector[last, row + 1 + step_x, col + 1 + step_y]
+                total = term if total is None else total + term
+            total = total * own_x[row, col]
+            crossing.append(tree([total[start : start + 8] for start in range(0, slots, 8)], jnp.add))
+    zero = jnp.zeros((8, slots), jnp.float32)
+    crossing = tree([(-one, zero) for one in crossing], add)
+    pair = over_sublanes(add(inside_sum, crossing), 8)
+    pair = sum_lanes(pair)
     gather_late[0, 0:1] = pair[0][0:1]
     gather_late[0, 1:2] = pair[1][0:1]
     start_all(*late_args)
 
+    end_product(last)
     end_all(*early_args)
     sums = {}
     for at in range(groups):
@@ -581,11 +611,13 @@
 
 
 def write_out(density_ref, pressure_ref, residual_ref, peaks_ref, *rest):
-    outs, sems = rest[:3], rest[4]
-    rest[3][...] = peaks_ref[0, : rest[3].shape[0]]
+    outs, packed_ref, sems = rest[:4], rest[4], rest[5]
+    packed_ref[...] = peaks_ref[0, : packed_ref.shape[0]]
     copies = [
         pltpu.make_async_copy(source, target, sems.at[index])
-        for index, (source, target) in enumerate(zip((density_ref, pressure_ref, residual_ref), outs))
+        for index, (source, target) in enumerate(
+            zip((density_ref, pressure_ref, residual_ref, packed_ref), outs)
+        )
     ]
     for copy in copies:
         copy.start()
@@ -601,8 +633,9 @@
     dma, f32, sides = pltpu.SemaphoreType.DMA, jnp.float32, len(SIDES)
     scratch = lambda *shape: pltpu.VMEM(shape, f32)
     early_rows = 2 * (-(-(ITERS * (ITERS + 1) // 2 - 1 + ITERS) // (slots // col_count)))
+    weight_bytes = 4 * row_count * col_count * len(NEIGHBOUR_STEPS) * slots * slots
     vmem = pl.BlockSpec(memory_space=pltpu.VMEM)
-    hbm = pl.BlockSpec(memory_space=pl.ANY)
+    hbm = pl.BlockSpec(memory_space=pltpu.HBM)
     shaped = jax.ShapeDtypeStruct(block, f32)
     results = pl.pallas_call(
         functools.partial(kernel, size_x, size_y, row_count, col_count),
@@ -627,14 +660,17 @@
             dma((devices,)), dma((devices,)), dma((devices,)), dma((devices,)),
             dma((devices,)), dma((devices,)),
         ],
-        compiler_params=pltpu.CompilerParams(collective_id=0, has_side_effects=True),
-    )(offsets, masses, counts, source)
+        compiler_params=pltpu.CompilerParams(
+            collective_id=0, has_side_effects=True, vmem_limit_bytes=3 * weight_bytes
+        ),
+    )(*(pltpu.with_memory_space_constraint(one, pltpu.HBM) for one in (offsets, masses, counts, source)))
     return pl.pallas_call(
         write_out,
         out_shape=(shaped, shaped, shaped, jax.ShapeDtypeStruct((ITERS,), f32)),
         in_specs=[vmem] * 4,
-        out_specs=(hbm, hbm, hbm, vmem),
-        scratch_shapes=[dma((3,))],
+        out_specs=(hbm,) * 4,
+        scratch_shapes=[scratch(ITERS), dma((4,))],
+        compiler_params=pltpu.CompilerParams(vmem_limit_bytes=weight_bytes),
     )(*results)
 
 

time: 44.1 us -> 41 us (0.930)
  Pallas kernels: 43 us -> 40.1 us
    pallas_call x1, Pallas kernels: 41.2 us -> 39.5 us  [body(): pl.pallas_call(functools.partial(kernel, size_x, size_y, row_count, col_c...]
    pallas_call x1, Pallas kernels: 1.88 us -> 0.65 us  [body(): pl.pallas_call(write_out, out_shape=(shaped, shaped, shaped, jax.ShapeDty...]
where the time goes in v2:
time: 41 us; the launch traced here: 40.8 us
  Pallas kernels  40.1 us (98%)
  between operations  0.64 us (2%)
    pallas_call x1, Pallas kernels, body(): pl.pallas_call(functools.partial(kernel, size_x, size_y, row_count, col_c...  39.5 us

profile of v2, /device:TPU:0, one launch (start us, length us, event | category | flops | bytes accessed | tf_op | source)
XLA Modules:
  0.0 40.8 jit_solution(9432260801369414689)
XLA Ops:
  0.6 39.5 %shard_map.75 = (f32[2,8,128]{2,1,0:T(8,128)S(1)}, f32[2,8,128]{2,1,0:T(8,128)S(1)}, f32[2,8,128]{2,1,0:T(8,128)S(1)}, f32[1,128]{1,0:T(1,128)S(1)}) custom-call(f32[2,2,8,128]{3,2,1,0:T(8,128)} %offsets_hbm.1, f32[2,8,128]{2,1,0:T(8,128)} %masses_hbm.1, s32[2,8]{1,0:T(2,128)} %counts_hbm.1, f32[2,8,128]{2,1,0:T(8,128)} %source_hbm.1), custom_call_target="tpu_custom_call" | custom-call | tf_op jit(solution)/shard_map/pallas_call | solution.py:640
  40.1 0.6 %shard_map.76 = (f32[2,8,128]{2,1,0:T(8,128)}, f32[2,8,128]{2,1,0:T(8,128)}, f32[2,8,128]{2,1,0:T(8,128)}, f32[5]{0:T(128)}) custom-call(f32[2,8,128]{2,1,0:T(8,128)S(1)} %get-tuple-element.8.density_ref, f32[2,8,128]{2,1,0:T(8,128)S(1)} %get-tuple-element.9.pressure_ref, f32[2,8,128]{2,1,0:T(8,128)S(1)} %get-tuple-element.10.residual_ref, ...), custom_call_target="tpu_custom_call" | custom-call | tf_op jit(solution)/shard_map/pallas_call | solution.py:667

commit v3 on v2

--- a/solution.py
+++ b/solution.py
@@ -16,6 +16,10 @@
 FAR = 64.0
 CENTRE, HALF = 0.4375, 0.5
 CHUNK = 64
+DEEP = (1, 3)
+READY = 9
+FIRST = 13
+MIDDLE = 0.5
 
 
 def two_sum(a, b):
@@ -87,9 +91,11 @@
     offsets_ref, masses_ref, counts_ref, source_ref, load_sem,
     pad_fields, pad_density, pad_vector, weights, own_x, own_y, own_density,
     part, inverse_diag, diag_ref, vectors, products, images,
+    deep_places, deep_density, ring_weights, ring_inverse, ring_part, ring_own,
     gather_early, gather_late, gather_peak,
     field_send, field_recv, density_send, density_recv, vector_send, vector_recv,
     early_send, early_recv, late_send, late_recv, peak_send, peak_recv,
+    deep_places_send, deep_places_recv, deep_density_send, deep_density_recv,
 ):
     here_x, here_y = lax.axis_index("gx"), lax.axis_index("gy")
     device_count = size_x * size_y
@@ -124,9 +130,15 @@
         return jnp.where(there >= size, there - size, there)
 
     def for_peers(action):
+        def turned(step_y):
+            return jnp.where(here_y < size_y // 2, size_y - step_y, step_y)
+
         if device_count <= 64:
-            for index in range(1, device_count):
-                action(index, index // size_y, index % size_y)
+            for step_y in range(1, size_y):
+                for step_x in range(size_x - 1, -1, -1):
+                    action(step_x * size_y + turned(step_y), step_x, turned(step_y))
+            for step_x in range(1, size_x):
+                action(step_x * size_y, step_x, 0)
         else:
             def one(index, carry):
                 action(index, lax.div(index, size_y), lax.rem(index, size_y))
@@ -139,10 +151,12 @@
     def greet(device):
         pl.semaphore_signal(barrier, inc=1, device_id=device, device_id_type=MESH)
 
-    near_only = max(size_x, size_y) <= ITERS + 3
+    near_only = size_x <= ITERS + 2 and size_y <= ITERS + 3
     if near_only:
         for step_x, step_y in SIDES:
             on_side(step_x, step_y, functools.partial(greet, (here_x + step_x, here_y + step_y)))
+        pl.when(here_y > 1)(lambda: greet((here_x, here_y - 2)))
+        pl.when(here_y < size_y - 2)(lambda: greet((here_x, here_y + 2)))
     else:
         for_peers(lambda index, step_x, step_y: greet(
             (ahead(here_x, step_x, size_x), ahead(here_y, step_y, size_y))
@@ -151,22 +165,35 @@
     def fill(ref, value):
         ref[...] = jnp.full(ref.shape, value, jnp.float32)
 
-    def fill_outside(at):
-        fill(pad_fields.at[at], FAR)
-        fill(pad_density.at[at], 0.0)
+    def fill_outside(axis, start):
+        def at(margin):
+            span = pl.ds(start + margin if start > 0 else 0, margin)
+            return (span, slice(None)) if axis == 0 else (slice(None), span)
+
+        fill(pad_fields.at[at(1)], FAR)
+        fill(pad_density.at[at(1)], 1.0)
+        fill(deep_places.at[at(2)], FAR)
+        fill(deep_density.at[at(2)], 1.0)
         for step in range(ITERS):
-            fill(pad_vector.at[(step,) + at], 0.0)
-
-    every = slice(None)
-    pl.when(jnp.logical_not(low_x))(lambda: fill_outside((0, every)))
-    pl.when(jnp.logical_not(high_x))(lambda: fill_outside((row_count + 1, every)))
-    pl.when(jnp.logical_not(low_y))(lambda: fill_outside((every, 0)))
-    pl.when(jnp.logical_not(high_y))(lambda: fill_outside((every, col_count + 1)))
-
-    def halo_copy(side, pad, send_sem, recv_sem):
+            fill(pad_vector.at[(step,) + at(2)], 0.0)
+
+    pl.when(jnp.logical_not(low_x))(lambda: fill_outside(0, 0))
+    pl.when(jnp.logical_not(high_x))(lambda: fill_outside(0, row_count))
+    pl.when(jnp.logical_not(low_y))(lambda: fill_outside(1, 0))
+    pl.when(jnp.logical_not(high_y))(lambda: fill_outside(1, col_count))
+
+    def halo_copy(side, pad, depth, send_sem, recv_sem):
         step_x, step_y = SIDES[side]
-        inner = lambda step, count: {1: pl.ds(count, 1), -1: pl.ds(1, 1), 0: pl.ds(1, count)}[step]
-        outer = lambda step, count: {1: pl.ds(0, 1), -1: pl.ds(count + 1, 1), 0: pl.ds(1, count)}[step]
+        margin = (pad.shape[0] - row_count) // 2
+
+        def inner(step, count):
+            start = margin + count - depth if step > 0 else margin
+            return pl.ds(start, depth if step else count)
+
+        def outer(step, count):
+            start = {1: margin - depth, -1: margin + count, 0: margin}[step]
+            return pl.ds(start, depth if step else count)
+
         return pltpu.make_async_remote_copy(
             src_ref=pad.at[inner(step_x, row_count), inner(step_y, col_count)],
             dst_ref=pad.at[outer(step_x, row_count), outer(step_y, col_count)],
@@ -200,29 +227,24 @@
         return [
             (index, step_x, step_y)
             for index, (step_x, step_y) in enumerate(NEIGHBOUR_STEPS)
-            if is_inside(step_x, step_y) == inside
+            if inside is None or is_inside(step_x, step_y) == inside
         ]
 
-    def edge_columns(action):
-        for col, place in ((0, "first"), (col_count - 1, "last")):
+    def columns(action, chosen):
+        for col in chosen:
+            place = "first" if col == 0 else "last" if col == col_count - 1 else "inner"
             for row in range(row_count):
                 action(row, col, place)
 
-    def inner_columns(action, unroll=True):
-        def one(col, carry):
-            for row in range(row_count):
-                action(row, col, "inner")
-            return carry
-
-        if unroll:
-            for col in range(1, col_count - 1):
-                one(col, 0)
-        else:
-            lax.fori_loop(1, col_count - 1, one, 0)
-
-    def all_columns(action, unroll=True):
+    def edge_columns(action, depth=1):
+        columns(action, [col for col in range(col_count) if not depth <= col < col_count - depth])
+
+    def inner_columns(action, depth=1):
+        columns(action, range(depth, col_count - depth))
+
+    def all_columns(action):
         edge_columns(action)
-        inner_columns(action, unroll)
+        inner_columns(action)
 
     def spread(row):
         return jnp.broadcast_to(row, (slots, slots)).T
@@ -234,6 +256,140 @@
         return gathered(jnp.concatenate(
             [terms(pl.ds(start, CHUNK)) for start in range(0, slots, CHUNK)], axis=0
         ))
+
+    wide = col_count + 2
+    ring = [(col + 1, -1, col) for col in range(-1, col_count + 1)]
+    ring += [(wide + col + 1, row_count, col) for col in range(-1, col_count + 1)]
+    ring += [(2 * wide + 2 * row, row, -1) for row in range(row_count)]
+    ring += [(2 * wide + 2 * row + 1, row, col_count) for row in range(row_count)]
+
+    ring_middle = [cell for cell in ring if 3 <= cell[2] < col_count - 3]
+    ring_ends = [cell for cell in ring if cell not in ring_middle]
+    ring_at = {(row, col): at for at, row, col in ring}
+
+    def known(at, row, col):
+        out = []
+        for index, (step_x, step_y) in enumerate(NEIGHBOUR_STEPS):
+            cell = (row + step_x, col + step_y)
+            back = len(NEIGHBOUR_STEPS) - 1 - index
+            if 0 <= cell[0] < row_count and 0 <= cell[1] < col_count:
+                out.append(("own", cell, back))
+            elif cell in ring_at and order[ring_at[cell]] < order[at]:
+                out.append(("ring", ring_at[cell], back))
+            else:
+                out.append(None)
+        return out
+
+    order = {at: place for place, (at, _, _) in enumerate(ring)}
+
+    def spread_ring_places(at, row, col):
+        places = deep_places[row + 2, col + 2]
+        ring_own[at, 0] = spread(2.0 * places[0:1])
+        ring_own[at, 1] = spread(2.0 * places[1:2])
+
+    def spread_ring(at, row, col):
+        if order[at] >= READY:
+            spread_ring_places(at, row, col)
+        ring_own[at, 2] = spread(deep_density[row + 2, col + 2])
+
+    def in_turn(prepare, action, cells):
+        prepare(*cells[0])
+        for place, cell in enumerate(cells):
+            if place + 1 < len(cells):
+                prepare(*cells[place + 1])
+            action(*cell)
+
+    def ring_squares(at, row, col, rows):
+        twice_x, twice_y = ring_own[at, 0, rows], ring_own[at, 1, rows]
+        rest = 1.0 - 0.25 * (twice_x * twice_x + twice_y * twice_y)
+
+        def one(index):
+            step_x, step_y = NEIGHBOUR_STEPS[index]
+            near = deep_places[row + 2 + step_x, col + 2 + step_y]
+            near_x, near_y = near[0:1] + step_x, near[1:2] + step_y
+            near_rest = near_x * near_x + near_y * near_y
+            falloff = (rest - near_rest) + (twice_x * near_x + twice_y * near_y)
+            falloff = jnp.maximum(falloff, 0.0)
+            return falloff * falloff
+
+        return one
+
+    def parts():
+        return [slice(start, start + CHUNK) for start in range(0, slots, CHUNK)]
+
+    def set_ring_squares(at, row, col):
+        for rows in parts():
+            squares = ring_squares(at, row, col, rows)
+            for index, found in enumerate(known(at, row, col)):
+                if found is None:
+                    ring_weights[at, index, rows] = squares(index)
+
+    def set_ring_weights(at, row, col):
+        ready = order[at] < READY
+        totals = []
+        turned = {}
+        for index, found in enumerate(known(at, row, col)):
+            if found is None:
+                continue
+            kind, cell, back = found
+            if kind == "own":
+                turned[index] = weights[cell[0], cell[1], back].T
+                places = deep_places[cell[0] + 2, cell[1] + 2]
+                live = (places[0:1] < FAR / 2).astype(jnp.float32)
+            else:
+                turned[index] = ring_weights[cell, back].T
+                live = 1.0
+            ring_weights[at, index] = turned[index]
+            turned[index] = turned[index] * live
+        for rows in parts():
+            squares = None if ready else ring_squares(at, row, col, rows)
+            here = ring_own[at, 2, rows]
+            total = None
+            for index, (step_x, step_y) in enumerate(NEIGHBOUR_STEPS):
+                if index in turned:
+                    weight = turned[index][rows]
+                else:
+                    there = deep_density[row + 2 + step_x, col + 2 + step_y]
+                    square = ring_weights[at, index, rows] if ready else squares(index)
+                    weight = square / (here + there)
+                    ring_weights[at, index, rows] = weight
+                total = weight if total is None else total + weight
+            totals.append(total)
+        total = gathered(jnp.concatenate(totals, axis=0))
+        live = (deep_places[row + 2, col + 2][0:1] < FAR / 2).astype(jnp.float32)
+        ring_inverse[at] = live / (BASE_STIFF + live * total)
+
+    def set_ring_share(step):
+        if step > DEEP[0]:
+            return
+        if step == 0:
+            end_halo(*deep_density_args)
+        share = ring[:FIRST] if step == 0 else ring[FIRST:]
+        in_turn(spread_ring, set_ring_weights, share)
+
+    def ring_product(step, at, row, col, inside):
+        total = None
+        for index, (step_x, step_y) in enumerate(NEIGHBOUR_STEPS):
+            own = 0 <= row + step_x < row_count and 0 <= col + step_y < col_count
+            if inside is None or own == inside:
+                term = ring_weights[at, index] * pad_vector[step, row + 2 + step_x, col + 2 + step_y]
+                total = term if total is None else total + term
+        return gathered(total)
+
+    def start_ring(step):
+        if step == DEEP[1]:
+            for at, row, col in ring:
+                ring_part[at] = ring_product(step, at, row, col, True)
+
+    def finish_ring(step, cells):
+        for at, row, col in cells:
+            if step == DEEP[1]:
+                product = ring_part[at] + ring_product(step, at, row, col, False)
+            else:
+                product = ring_product(step, at, row, col, None)
+            rest = ring_inverse[at] * product - CENTRE * pad_vector[step, row + 2, col + 2]
+            following = rest * (2.0 / HALF) - pad_vector[step - 1, row + 2, col + 2]
+            pad_vector[step + 1, row + 2, col + 2] = following
 
     for load in loads:
         load.wait()
@@ -258,17 +414,23 @@
         for col in range(col_count):
             for index in range(3):
                 pad_fields[row + 1, col + 1, index : index + 1] = field_rows[index][col : col + 1]
+            for index in range(2):
+                centred = field_rows[index][col : col + 1] - MIDDLE
+                deep_places[row + 2, col + 2, index : index + 1] = centred
         inverse_diag[row] = occupied[row].reshape(col_count, 1, slots)
 
     greeters = lambda low, high: low.astype(jnp.int32) + high.astype(jnp.int32)
     if near_only:
         count_x, count_y = greeters(low_x, high_x), greeters(low_y, high_y)
-        pl.semaphore_wait(barrier, (count_x + 1) * (count_y + 1) - 1)
+        further = greeters(here_y > 1, here_y < size_y - 2)
+        pl.semaphore_wait(barrier, (count_x + 1) * (count_y + 1) - 1 + further)
     else:
         pl.semaphore_wait(barrier, device_count - 1)
 
-    field_args = (pad_fields, field_send, field_recv)
+    field_args = (pad_fields, 1, field_send, field_recv)
     start_halo(range(len(SIDES)), *field_args)
+    deep_places_args = (deep_places, 2, deep_places_send, deep_places_recv)
+    start_halo(range(len(SIDES)), *deep_places_args)
 
     def spread_place(row, col, place):
         own_x[row, col] = spread(offsets_ref[0, row, pl.ds(col, 1)])
@@ -307,13 +469,16 @@
     def finish_density(row, col, place):
         density = 1.0 + (part[row, col] + density_part(False)(row, col, place))
         pad_density[row + 1, col + 1] = density
+        deep_density[row + 2, col + 2] = density * (0.5 / PAIR_SCALE)
         density_ref[row, pl.ds(col, 1)] = density
 
-    density_args = (pad_density, density_send, density_recv)
+    density_args = (pad_density, 1, density_send, density_recv)
+    deep_density_args = (deep_density, 2, deep_density_send, deep_density_recv)
     edge_columns(finish_density)
     start_halo(LONG, *density_args)
     inner_columns(finish_density)
     start_halo(SHORT, *density_args)
+    start_halo(range(len(SIDES)), *deep_density_args)
 
     def weight_part(inside):
         def one(row, col, place):
@@ -338,6 +503,8 @@
         part[row, col] = weight_part(True)(row, col, place)
 
     all_columns(store_weight_part)
+    end_halo(*deep_places_args)
+    in_turn(spread_ring_places, set_ring_squares, ring[:READY])
     end_halo(*density_args)
 
     def finish_weights(row, col, place):
@@ -349,10 +516,11 @@
         diag_ref[row, pl.ds(col, 1)] = diagonal
         inverse_diag[row, col] = inverted
         vectors[0, row, pl.ds(col, 1)] = scaled
-        pad_vector[0, row + 1, col + 1] = scaled
+        pad_vector[0, row + 2, col + 2] = scaled
 
     def vector_args(step):
-        return pad_vector.at[step], vector_send.at[step], vector_recv.at[step]
+        depth = 2 if step in DEEP else 1
+        return pad_vector.at[step], depth, vector_send.at[step], vector_recv.at[step]
 
     edge_columns(finish_weights)
     start_halo(LONG, *vector_args(0))
@@ -363,7 +531,7 @@
         def one(row, col, place):
             total = None
             for index, step_x, step_y in steps_of(row, place, inside):
-                term = weights[row, col, index] * pad_vector[step, row + 1 + step_x, col + 1 + step_y]
+                term = weights[row, col, index] * pad_vector[step, row + 2 + step_x, col + 2 + step_y]
                 total = term if total is None else total + term
             return gathered(total)
 
@@ -377,7 +545,10 @@
 
     def finish_product(step):
         def one(row, col, place):
-            product = part[row, col] + product_part(step, False)(row, col, place)
+            if step - 1 in DEEP:
+                product = product_part(step, None)(row, col, place)
+            else:
+                product = part[row, col] + product_part(step, False)(row, col, place)
             products[step, row, pl.ds(col, 1)] = product
             now = vectors[step, row, pl.ds(col, 1)]
             rest = inverse_diag[row, col] * product - CENTRE * now
@@ -387,7 +558,7 @@
                 following = rest * (2.0 / HALF) - vectors[step - 1, row, pl.ds(col, 1)]
             vectors[step + 1, row, pl.ds(col, 1)] = following
             if step + 1 < ITERS:
-                pad_vector[step + 1, row + 1, col + 1] = following
+                pad_vector[step + 1, row + 2, col + 2] = following
 
         return one
 
@@ -426,18 +597,24 @@
     peak_args = (gather_peak, peak_send, peak_recv)
     last = ITERS - 1
     group = slots // col_count
-    entries = [("image", i, j) for j in range(ITERS) for i in range(j + 1) if i < last]
-    entries += [("source", 0, j) for j in range(ITERS)]
+    entries = [("image", i, j) for j in range(last) for i in range(min(j + 1, last - 1))]
+    entries += [("source", 0, j) for j in range(last)]
+    late_entries = [("image", last - 1, last - 1), ("source", 0, last)]
+    late_entries += [("image", i, last) for i in range(last)]
+    entries += [None] * (-len(entries) % group) + late_entries
     groups = -(-len(entries) // group)
-
-    def early_sums():
-        pairs = []
-        for kind, i, j in entries:
-            left = images.at[i] if kind == "image" else source_ref
-            pairs.append(dot(left, vectors.at[j]))
+    first_late = groups - -(-len(late_entries) // group)
+
+    def early_sums(chosen):
         filler = jnp.zeros((col_count, slots), jnp.float32)
-        for at in range(groups):
-            rows = pairs[at * group : (at + 1) * group]
+        for at in chosen:
+            rows = []
+            for entry in entries[at * group : (at + 1) * group]:
+                if entry is None:
+                    rows.append((filler, filler))
+                    continue
+                kind, i, j = entry
+                rows.append(dot(images.at[i] if kind == "image" else source_ref, vectors.at[j]))
             rows = rows + [(filler, filler)] * (group - len(rows))
             flat = [jnp.concatenate([pair[which] for pair in rows], axis=0).T for which in (0, 1)]
             slabs = [
@@ -453,43 +630,57 @@
         return over_sublanes(tree(slabs, add), 8)
 
     def end_product(step):
-        edge_columns(finish_product(step))
+        sends = step < last and step not in DEEP
+        depth = 2 if step + 1 in DEEP else 1
+        edge_columns(finish_product(step), depth)
+        if sends:
+            start_halo(LONG, *vector_args(step + 1))
+        if step - 1 in DEEP and sends:
+            finish_ring(step - 1, ring_middle)
+        inner_columns(finish_product(step), depth)
+        if sends:
+            start_halo(SHORT, *vector_args(step + 1))
         if step < last:
-            start_halo(LONG, *vector_args(step + 1))
-        inner_columns(finish_product(step))
-        if step < last:
-            start_halo(SHORT, *vector_args(step + 1))
             set_image(step)
 
     for step in range(last):
-        all_columns(store_product_part(step))
-        end_halo(*vector_args(step))
+        if step - 1 not in DEEP:
+            all_columns(store_product_part(step))
+            set_ring_share(step)
+            if step == DEEP[1]:
+                early_sums(range(first_late))
+            start_ring(step)
+            end_halo(*vector_args(step))
         end_product(step)
-    early_sums()
-    start_all(*early_args)
-    all_columns(store_product_part(last))
-
-    for row in range(row_count):
-        for col in range(col_count):
-            own_x[row, col] = spread(vectors[last, row, pl.ds(col, 1)])
-            products[last, row, pl.ds(col, 1)] = part[row, col]
-    set_image(last)
-    inside_sum = dot(images.at[last], vectors.at[last])
-    end_halo(*vector_args(last))
+        if step == last - 1:
+            early_sums(range(first_late, groups))
+            start_all(*early_args)
+        if step in DEEP:
+            finish_ring(step, ring_ends if step == DEEP[0] else ring)
+
     crossing = []
     for row in range(row_count):
         for col in range(col_count):
             place = "first" if col == 0 else "last" if col == col_count - 1 else "inner"
-            total = None
-            for index, step_x, step_y in steps_of(row, place, False):
-                term = weights[row, col, index] * pad_vector[last, row + 1 + step_x, col + 1 + step_y]
-                total = term if total is None else total + term
-            total = total * own_x[row, col]
+            inside = [index for index, _, _ in steps_of(row, place, True)]
+            single = twice = None
+            for index, (step_x, step_y) in enumerate(NEIGHBOUR_STEPS):
+                if index in inside and (step_x, step_y) < (0, 0):
+                    continue
+                term = weights[row, col, index] * pad_vector[last, row + 2 + step_x, col + 2 + step_y]
+                if index in inside and (step_x, step_y) > (0, 0):
+                    twice = term if twice is None else twice + term
+                else:
+                    single = term if single is None else single + term
+            total = single if twice is None else single + (twice + twice)
+            total = total * spread(vectors[last, row, pl.ds(col, 1)])
             crossing.append(tree([total[start : start + 8] for start in range(0, slots, 8)], jnp.add))
     zero = jnp.zeros((8, slots), jnp.float32)
-    crossing = tree([(-one, zero) for one in crossing], add)
-    pair = over_sublanes(add(inside_sum, crossing), 8)
-    pair = sum_lanes(pair)
+    pair = tree([(-one, zero) for one in crossing], add)
+    for row in range(row_count):
+        now = vectors[last, row]
+        pair = add(pair, (diag_ref[row] * now * now, zero))
+    pair = sum_lanes(over_sublanes(pair, 8))
     gather_late[0, 0:1] = pair[0][0:1]
     gather_late[0, 1:2] = pair[1][0:1]
     start_all(*late_args)
@@ -507,6 +698,8 @@
         )
         flat = [spread(part_of) for part_of in pair]
         for index, entry in enumerate(entries[at * group : (at + 1) * group]):
+            if entry is None:
+                continue
             rows = slice(index * col_count, (index + 1) * col_count)
             sums[entry] = tidy(over_sublanes((flat[0][rows], flat[1][rows]), col_count))
     matrix = lambda i, j: sums["image", min(i, j), max(i, j)]
@@ -601,8 +794,11 @@
 
     end_sends(*field_args)
     end_sends(*density_args)
+    end_sends(*deep_places_args)
+    end_sends(*deep_density_args)
     for step in range(ITERS):
-        end_sends(*vector_args(step))
+        if step - 1 not in DEEP:
+            end_sends(*vector_args(step))
     end_all_sends(*early_args)
     end_all_sends(*late_args)
     end_all(*peak_args)
@@ -629,10 +825,13 @@
     row_count, col_count, slots = masses.shape
     devices = size_x * size_y
     padded = (row_count + 2, col_count + 2)
+    deep = (row_count + 4, col_count + 4)
+    ring_count = padded[0] * padded[1] - row_count * col_count
     block = (row_count, col_count, slots)
     dma, f32, sides = pltpu.SemaphoreType.DMA, jnp.float32, len(SIDES)
     scratch = lambda *shape: pltpu.VMEM(shape, f32)
-    early_rows = 2 * (-(-(ITERS * (ITERS + 1) // 2 - 1 + ITERS) // (slots // col_count)))
+    group = slots // col_count
+    early_rows = 2 * (-(-((ITERS - 1) * (ITERS + 2) // 2 - 1) // group) + -(-(ITERS + 1) // group))
     weight_bytes = 4 * row_count * col_count * len(NEIGHBOUR_STEPS) * slots * slots
     vmem = pl.BlockSpec(memory_space=pltpu.VMEM)
     hbm = pl.BlockSpec(memory_space=pltpu.HBM)
@@ -645,7 +844,7 @@
         scratch_shapes=[
             scratch(2, *block), scratch(*block), pltpu.VMEM((row_count, col_count), jnp.int32),
             scratch(*block), dma((4,)),
-            scratch(*padded, 4, slots), scratch(*padded, 1, slots), scratch(ITERS, *padded, 1, slots),
+            scratch(*padded, 4, slots), scratch(*padded, 1, slots), scratch(ITERS, *deep, 1, slots),
             scratch(row_count, col_count, len(NEIGHBOUR_STEPS), slots, slots),
             scratch(row_count, col_count, slots, slots),
             scratch(row_count, col_count, slots, slots),
@@ -654,14 +853,18 @@
             scratch(row_count, col_count, 1, slots),
             scratch(*block),
             scratch(ITERS + 1, *block), scratch(ITERS, *block), scratch(ITERS, *block),
+            scratch(*deep, 2, slots), scratch(*deep, 1, slots),
+            scratch(ring_count, len(NEIGHBOUR_STEPS), slots, slots), scratch(ring_count, 1, slots),
+            scratch(ring_count, 1, slots), scratch(ring_count, 3, slots, slots),
             scratch(devices, early_rows, slots), scratch(devices, 2, slots), scratch(devices, 1, slots),
             dma((sides,)), dma((sides,)), dma((sides,)), dma((sides,)),
             dma((ITERS, sides)), dma((ITERS, sides)),
             dma((devices,)), dma((devices,)), dma((devices,)), dma((devices,)),
             dma((devices,)), dma((devices,)),
+            dma((sides,)), dma((sides,)), dma((sides,)), dma((sides,)),
         ],
         compiler_params=pltpu.CompilerParams(
-            collective_id=0, has_side_effects=True, vmem_limit_bytes=3 * weight_bytes
+            collective_id=0, has_side_effects=True, vmem_limit_bytes=4 * weight_bytes
         ),
     )(*(pltpu.with_memory_space_constraint(one, pltpu.HBM) for one in (offsets, masses, counts, source)))
     return pl.pallas_call(

time: 41 us -> 38.4 us (0.937)
  Pallas kernels: 40.1 us -> 37.3 us
    pallas_call x1, Pallas kernels: 39.5 us -> 36.7 us  [body(): pl.pallas_call(functools.partial(kernel, size_x, size_y, row_count, col_c...]
where the time goes in v3:
time: 38.4 us; the launch traced here: 38.1 us
  Pallas kernels  37.3 us (97%)
  between operations  0.8 us (2%)
    pallas_call x1, Pallas kernels, body(): pl.pallas_call(functools.partial(kernel, size_x, size_y, row_count, col_c...  36.7 us

profile of v3, /device:TPU:0, one launch (start us, length us, event | category | flops | bytes accessed | tf_op | source)
XLA Modules:
  0.0 38.1 jit_solution(5476114371923650114)
XLA Ops:
  0.6 36.7 %shard_map.75 = (f32[2,8,128]{2,1,0:T(8,128)S(1)}, f32[2,8,128]{2,1,0:T(8,128)S(1)}, f32[2,8,128]{2,1,0:T(8,128)S(1)}, f32[1,128]{1,0:T(1,128)S(1)}) custom-call(f32[2,2,8,128]{3,2,1,0:T(8,128)} %offsets_hbm.1, f32[2,8,128]{2,1,0:T(8,128)} %masses_hbm.1, s32[2,8]{1,0:T(2,128)} %counts_hbm.1, f32[2,8,128]{2,1,0:T(8,128)} %source_hbm.1), custom_call_target="tpu_custom_call" | custom-call | tf_op jit(solution)/shard_map/pallas_call | solution.py:839
  37.3 0.6 %shard_map.76 = (f32[2,8,128]{2,1,0:T(8,128)}, f32[2,8,128]{2,1,0:T(8,128)}, f32[2,8,128]{2,1,0:T(8,128)}, f32[5]{0:T(128)}) custom-call(f32[2,8,128]{2,1,0:T(8,128)S(1)} %get-tuple-element.8.density_ref, f32[2,8,128]{2,1,0:T(8,128)S(1)} %get-tuple-element.9.pressure_ref, f32[2,8,128]{2,1,0:T(8,128)S(1)} %get-tuple-element.10.residual_ref, ...), custom_call_target="tpu_custom_call" | custom-call | tf_op jit(solution)/shard_map/pallas_call | solution.py:870

commit v4 on v3

--- a/solution.py
+++ b/solution.py
@@ -17,6 +17,7 @@
 CENTRE, HALF = 0.4375, 0.5
 CHUNK = 64
 DEEP = (1, 3)
+SHORT_WAY, LONG_WAY = "short", "long"
 READY = 9
 FIRST = 13
 MIDDLE = 0.5
@@ -210,8 +211,9 @@
         for side in sides:
             on_side(*SIDES[side], lambda side=side: halo_copy(side, *args).start())
 
-    def end_halo(*args):
-        for side, (step_x, step_y) in enumerate(SIDES):
+    def end_halo(*args, sides=range(len(SIDES))):
+        for side in sides:
+            step_x, step_y = SIDES[side]
             on_side(-step_x, -step_y, lambda side=side: halo_copy(side, *args).wait_recv())
 
     def end_sends(*args):
@@ -224,10 +226,16 @@
                 return False
             return not (place == "first" and step_y < 0 or place == "last" and step_y > 0)
 
+        def is_wanted(step_x, step_y):
+            if inside in (SHORT_WAY, LONG_WAY):
+                long_way = place == "first" and step_y < 0 or place == "last" and step_y > 0
+                return not is_inside(step_x, step_y) and long_way == (inside == LONG_WAY)
+            return inside is None or is_inside(step_x, step_y) == inside
+
         return [
             (index, step_x, step_y)
             for index, (step_x, step_y) in enumerate(NEIGHBOUR_STEPS)
-            if inside is None or is_inside(step_x, step_y) == inside
+            if is_wanted(step_x, step_y)
         ]
 
     def columns(action, chosen):
@@ -265,6 +273,10 @@
 
     ring_middle = [cell for cell in ring if 3 <= cell[2] < col_count - 3]
     ring_ends = [cell for cell in ring if cell not in ring_middle]
+    ring_short = [
+        cell for cell in ring if cell[1] in (-1, row_count) and 1 <= cell[2] < col_count - 1
+    ]
+    ring_long = [cell for cell in ring if cell not in ring_short]
     ring_at = {(row, col): at for at, row, col in ring}
 
     def known(at, row, col):
@@ -463,11 +475,17 @@
     def store_density_part(row, col, place):
         part[row, col] = density_part(True)(row, col, place)
 
+    def add_density_part(row, col, place):
+        part[row, col] = part[row, col] + density_part(SHORT_WAY)(row, col, place)
+
     all_columns(store_density_part)
-    end_halo(*field_args)
+    end_halo(*field_args, sides=SHORT)
+    edge_columns(add_density_part)
+    end_halo(*field_args, sides=LONG)
 
     def finish_density(row, col, place):
-        density = 1.0 + (part[row, col] + density_part(False)(row, col, place))
+        rest = density_part(False if place == "inner" else LONG_WAY)(row, col, place)
+        density = 1.0 + (part[row, col] + rest)
         pad_density[row + 1, col + 1] = density
         deep_density[row + 2, col + 2] = density * (0.5 / PAIR_SCALE)
         density_ref[row, pl.ds(col, 1)] = density
@@ -632,12 +650,17 @@
     def end_product(step):
         sends = step < last and step not in DEEP
         depth = 2 if step + 1 in DEEP else 1
+        if step == DEEP[1]:
+            inner_columns(finish_product(step), depth)
+            finish_ring(step, ring_short)
+            end_halo(*vector_args(step), sides=LONG)
         edge_columns(finish_product(step), depth)
         if sends:
             start_halo(LONG, *vector_args(step + 1))
         if step - 1 in DEEP and sends:
             finish_ring(step - 1, ring_middle)
-        inner_columns(finish_product(step), depth)
+        if step != DEEP[1]:
+            inner_columns(finish_product(step), depth)
         if sends:
             start_halo(SHORT, *vector_args(step + 1))
         if step < last:
@@ -650,13 +673,16 @@
             if step == DEEP[1]:
                 early_sums(range(first_late))
             start_ring(step)
-            end_halo(*vector_args(step))
+            if step == DEEP[1]:
+                end_halo(*vector_args(step), sides=SHORT)
+            else:
+                end_halo(*vector_args(step))
         end_product(step)
         if step == last - 1:
             early_sums(range(first_late, groups))
             start_all(*early_args)
         if step in DEEP:
-            finish_ring(step, ring_ends if step == DEEP[0] else ring)
+            finish_ring(step, ring_ends if step == DEEP[0] else ring_long)
 
     crossing = []
     for row in range(row_count):

time: 38.4 us -> 38 us (0.990)
  Pallas kernels: 37.3 us -> 36.9 us
    pallas_call x1, Pallas kernels: 36.7 us -> 36.3 us  [body(): pl.pallas_call(functools.partial(kernel, size_x, size_y, row_count, col_c...]
where the time goes in v4:
time: 38 us; the launch traced here: 37.7 us
  Pallas kernels  36.9 us (97%)
  between operations  0.8 us (2%)
    pallas_call x1, Pallas kernels, body(): pl.pallas_call(functools.partial(kernel, size_x, size_y, row_count, col_c...  36.3 us

profile of v4, /device:TPU:0, one launch (start us, length us, event | category | flops | bytes accessed | tf_op | source)
XLA Modules:
  0.0 37.7 jit_solution(17671131068386889550)
XLA Ops:
  0.6 36.3 %shard_map.75 = (f32[2,8,128]{2,1,0:T(8,128)S(1)}, f32[2,8,128]{2,1,0:T(8,128)S(1)}, f32[2,8,128]{2,1,0:T(8,128)S(1)}, f32[1,128]{1,0:T(1,128)S(1)}) custom-call(f32[2,2,8,128]{3,2,1,0:T(8,128)} %offsets_hbm.1, f32[2,8,128]{2,1,0:T(8,128)} %masses_hbm.1, s32[2,8]{1,0:T(2,128)} %counts_hbm.1, f32[2,8,128]{2,1,0:T(8,128)} %source_hbm.1), custom_call_target="tpu_custom_call" | custom-call | tf_op jit(solution)/shard_map/pallas_call | solution.py:865
  36.9 0.6 %shard_map.76 = (f32[2,8,128]{2,1,0:T(8,128)}, f32[2,8,128]{2,1,0:T(8,128)}, f32[2,8,128]{2,1,0:T(8,128)}, f32[5]{0:T(128)}) custom-call(f32[2,8,128]{2,1,0:T(8,128)S(1)} %get-tuple-element.8.density_ref, f32[2,8,128]{2,1,0:T(8,128)S(1)} %get-tuple-element.9.pressure_ref, f32[2,8,128]{2,1,0:T(8,128)S(1)} %get-tuple-element.10.residual_ref, ...), custom_call_target="tpu_custom_call" | custom-call | tf_op jit(solution)/shard_map/pallas_call | solution.py:896

commit v5 on v4

--- a/solution.py
+++ b/solution.py
@@ -14,7 +14,7 @@
 SIDES = [step for step in NEIGHBOUR_STEPS if step != (0, 0)]
 MESH = pl.DeviceIdType.MESH
 FAR = 64.0
-CENTRE, HALF = 0.4375, 0.5
+NODES, SCALE = (0.0, 0.875, 0.4375, 0.1875, 0.6875), 0.5
 CHUNK = 64
 DEEP = (1, 3)
 SHORT_WAY, LONG_WAY = "short", "long"
@@ -399,8 +399,8 @@
                 product = ring_part[at] + ring_product(step, at, row, col, False)
             else:
                 product = ring_product(step, at, row, col, None)
-            rest = ring_inverse[at] * product - CENTRE * pad_vector[step, row + 2, col + 2]
-            following = rest * (2.0 / HALF) - pad_vector[step - 1, row + 2, col + 2]
+            rest = ring_inverse[at] * product - NODES[step] * pad_vector[step, row + 2, col + 2]
+            following = rest * (1.0 / SCALE)
             pad_vector[step + 1, row + 2, col + 2] = following
 
     for load in loads:
@@ -569,11 +569,7 @@
                 product = part[row, col] + product_part(step, False)(row, col, place)
             products[step, row, pl.ds(col, 1)] = product
             now = vectors[step, row, pl.ds(col, 1)]
-            rest = inverse_diag[row, col] * product - CENTRE * now
-            if step == 0:
-                following = rest * (1.0 / HALF)
-            else:
-                following = rest * (2.0 / HALF) - vectors[step - 1, row, pl.ds(col, 1)]
+            following = (inverse_diag[row, col] * product - NODES[step] * now) * (1.0 / SCALE)
             vectors[step + 1, row, pl.ds(col, 1)] = following
             if step + 1 < ITERS:
                 pad_vector[step + 1, row + 2, col + 2] = following
@@ -764,13 +760,9 @@
 
     def applied(direction):
         count = len(direction)
-        padded = direction + [nothing, nothing]
-        out = []
-        for i in range(count + 1):
-            value = mul(padded[i], number(1.0 - CENTRE))
-            if i:
-                value = sub(value, mul(padded[i - 1], number(HALF if i == 1 else HALF / 2)))
-            out.append(sub(value, mul(padded[i + 1], number(HALF / 2))))
+        out = [mul(value, number(1.0 - NODES[i])) for i, value in enumerate(direction)] + [nothing]
+        for i in range(count):
+            out[i + 1] = sub(out[i + 1], mul(direction[i], number(SCALE)))
         return out
 
     def combined(coefficients, row):

time: 38 us -> 37.9 us (level)
  no operation moved by 1% of the time
where the time goes in v5:
time: 37.9 us; the launch traced here: 37.7 us
  Pallas kernels  36.9 us (97%)
  between operations  0.8 us (2%)
    pallas_call x1, Pallas kernels, body(): pl.pallas_call(functools.partial(kernel, size_x, size_y, row_count, col_c...  36.3 us

profile of v5, /device:TPU:0, one launch (start us, length us, event | category | flops | bytes accessed | tf_op | source)
XLA Modules:
  0.0 37.7 jit_solution(926135490555344083)
XLA Ops:
  0.6 36.3 %shard_map.75 = (f32[2,8,128]{2,1,0:T(8,128)S(1)}, f32[2,8,128]{2,1,0:T(8,128)S(1)}, f32[2,8,128]{2,1,0:T(8,128)S(1)}, f32[1,128]{1,0:T(1,128)S(1)}) custom-call(f32[2,2,8,128]{3,2,1,0:T(8,128)} %offsets_hbm.1, f32[2,8,128]{2,1,0:T(8,128)} %masses_hbm.1, s32[2,8]{1,0:T(2,128)} %counts_hbm.1, f32[2,8,128]{2,1,0:T(8,128)} %source_hbm.1), custom_call_target="tpu_custom_call" | custom-call | tf_op jit(solution)/shard_map/pallas_call | solution.py:857
  36.9 0.6 %shard_map.76 = (f32[2,8,128]{2,1,0:T(8,128)}, f32[2,8,128]{2,1,0:T(8,128)}, f32[2,8,128]{2,1,0:T(8,128)}, f32[5]{0:T(128)}) custom-call(f32[2,8,128]{2,1,0:T(8,128)S(1)} %get-tuple-element.8.density_ref, f32[2,8,128]{2,1,0:T(8,128)S(1)} %get-tuple-element.9.pressure_ref, f32[2,8,128]{2,1,0:T(8,128)S(1)} %get-tuple-element.10.residual_ref, ...), custom_call_target="tpu_custom_call" | custom-call | tf_op jit(solution)/shard_map/pallas_call | solution.py:888
